TPU v7x, 32 devices: a whole 2x2x4 slice. The times are simulated.
32 devices in a mesh: rows: 8 (over z, y), cols: 4 (over x, core).
Axes of the slice: x: 2, y: 2, z: 4, core: 2. Of those that a mesh axis runs over, the one named last changes fastest.
Arguments:
- tile_values: bfloat16 [8, 4, 320, 128, 128], P('rows', 'cols'), may hold values from -0.0625 to 0.0625
- tile_rows: int32 [8, 4, 320], P('rows', 'cols'), may hold values from 0 to 7
- tile_cols: int32 [8, 4, 320], P('rows', 'cols'), may hold values from 0 to 15
- tile_counts: int32 [8, 4], P('rows', 'cols'), may hold values from 1 to 320, as said below
- sketch: bfloat16 [8192, 160], P(('rows', 'cols')), may hold values from -6 to 6
Outputs:
- basis: float32 [8192, 160], P(('rows', 'cols'))
- factor: float32 [160, 160], replicated
Inputs may be any that keep to these rules, and one draw needn't show every extreme that they name: Only the first tile_counts[r, c] slots of list (r, c) are live; some list has all 320 slots live in every draw. `tile_cols`: the same place may stand in several live slots of a list.
All inputs are finite; a program needn't handle non-finite values.
Results may differ from a plain program's by a relative error of at most 0.0029.
Values may be sent and summed in bfloat16 or wider, within the bound.
A program may use at most 128 MiB of HBM per device.

v0:
```python
import math
import jax
import jax.numpy as jnp
from jax import lax
from jax.sharding import PartitionSpec as P

POWER = 2
RT = 8


def accumulate(block_list, row_list, col_list, live_count, gathered, height):
    slot_total = block_list.shape[0]
    tile_size = block_list.shape[1]
    sketch_width = gathered.shape[1]
    tile_stack = gathered.reshape(-1, tile_size, sketch_width)
    block_size = math.gcd(32, slot_total)

    def one_block(block_index, running):
        first_slot = block_index * block_size
        block_values = lax.dynamic_slice_in_dim(block_list, first_slot, block_size, 0)
        rowids = lax.dynamic_slice_in_dim(row_list, first_slot, block_size, 0)
        colids = lax.dynamic_slice_in_dim(col_list, first_slot, block_size, 0)
        picked = jnp.take(tile_stack, colids, axis=0)
        products = jnp.einsum(
            "sab,sbk->sak", block_values, picked, preferred_element_type=jnp.float32
        )
        live_mask = (first_slot + jnp.arange(block_size, dtype=jnp.int32) < live_count).astype(
            jnp.float32
        )
        return running.at[rowids].add(products * live_mask[:, None, None])

    block_count = (live_count + block_size - 1) // block_size
    initial = jnp.zeros((height, tile_size, sketch_width), jnp.float32)
    running = lax.fori_loop(0, block_count, one_block, initial)
    return running.reshape(height * tile_size, sketch_width)


def shards(tile_values, tile_rows, tile_cols, tile_counts, sketch):
    own_values = tile_values[0, 0]
    own_rows = tile_rows[0, 0]
    own_cols = tile_cols[0, 0]
    own_count = tile_counts[0, 0]
    nodes_total = sketch.shape[0] * lax.axis_size("rows") * lax.axis_size("cols")
    current = sketch
    solved = None
    factor = None
    for power in range(POWER):
        gathered = lax.all_gather(current, "rows", axis=0, tiled=True)
        partial_value = accumulate(own_values, own_rows, own_cols, own_count, gathered, RT)
        whole = lax.psum(partial_value, "cols")
        gram_matrix = lax.psum(jnp.dot(whole.T, whole, precision=lax.Precision.HIGHEST), "rows")
        share_rows = whole.shape[0] // lax.axis_size("cols")
        owned = lax.dynamic_slice_in_dim(whole, lax.axis_index("cols") * share_rows, share_rows, 0)
        gram_matrix = gram_matrix / nodes_total
        factor = jnp.linalg.cholesky(gram_matrix)
        solved = lax.linalg.triangular_solve(
            factor, owned, left_side=False, lower=True, transpose_a=True
        )
        current = solved.astype(jnp.bfloat16)
    return (solved, factor)


def solution(mesh):
    placed = (
        P("rows", "cols", None, None, None),
        P("rows", "cols", None),
        P("rows", "cols", None),
        P("rows", "cols"),
        P(("rows", "cols"), None),
    )
    return jax.shard_map(
        shards,
        mesh=mesh,
        in_specs=placed,
        out_specs=(P(("rows", "cols"), None), P()),
        check_vma=False,
    )
```

profile of v0, /device:TPU:0, one launch (start us, length us, event | category | flops | bytes accessed | tf_op | source)
XLA Modules:
  0.0 597.8 jit_solution(8288383398452547619)
XLA Ops:
  9.3 33.6 %all_gather.6 = bf16[2048,160]{0,1:T(8,128)(2,1)S(1)} all-gather(bf16[256,160]{0,1:T(8,128)(2,1)} %param.18), channel_id=1, replica_groups=mesh['rows'=8,'cols'=4] {'rows'}, dimensions={0}, use_global_device_ids=true | all-gather | bytes 737280 | tf_op jit(solution)/shard_map/all_gather | solution.py:48
  42.9 1.3 copy.17
  44.2 19.8 %while.23 = (s32[]{:T(128)}, f32[8,128,160]{1,2,0:T(8,128)S(1)}, s32[]{:T(128)}, s32[320]{0:T(512)S(1)}, bf16[320,128,128]{2,1,0:T(8,128)(2,1)}, /*index=5*/s32[...) while((s32[]{:T(128)}, f32[8,128,160]{1,2,0:T(8,128)S(1)}, ...), condition=%wide.region_2.4_spmd, body=%wide.region_0.3_spmd.sunk | while | flops 169739648 | bytes 16258423 | solution.py:34
  45.0 3.3 gather_fusion
  48.3 2.8 fusion.69
  51.1 3.0 scatter_fusion
  54.9 3.3 gather_fusion
  58.1 2.8 fusion.69
  61.0 3.0 scatter_fusion
  65.0 110.6 %all-reduce.8.cloned.1.call-done = f32[1024,160]{0,1:T(8,128)} async-done(((f32[1024,160]{0,1:T(8,128)}), f32[1024,160]{0,1:T(8,128)}) %all-reduce.8.cloned.1.call-update) | async-done | bytes 655376 | tf_op jit(solution)/shard_map/psum | solution.py:50
  175.6 2.6 fusion.45
  178.6 71.0 %all-reduce.10.cloned.1.call-done = f32[160,160]{0,1:T(8,128)} async-done(((f32[160,160]{0,1:T(8,128)}), f32[160,160]{0,1:T(8,128)}) %all-reduce.10.cloned.1.call-update) | async-done | bytes 102416 | tf_op jit(solution)/shard_map/psum | solution.py:51
  251.6 11.7 %cholesky.136 = f32[128,128]{1,0:T(8,128)S(1)} custom-call(f32[128,128]{1,0:T(8,128)S(1)} %cholesky.208), custom_call_target="Cholesky" | custom-call | tf_op jit(solution)/shard_map/jit(cholesky)/cholesky | solution.py:55
  263.4 9.8 %custom-call.13 = f32[1,128,128]{1,2,0:T(8,128)S(1)} custom-call(f32[1,128,128]{2,1,0:T(8,128)S(1)} %get-tuple-element.178), custom_call_target="InvertDiagBlocksLowerTriangular" | custom-call | tf_op jit(solution)/shard_map/jit(cholesky)/cholesky | solution.py:55
  273.5 2.9 cholesky.156
  279.2 19.7 %custom-call.14 = f32[2,128,128]{1,2,0:T(8,128)S(1)} custom-call(f32[2,128,128]{2,1,0:T(8,128)S(1)} %pad_maximum_fusion.1), custom_call_target="InvertDiagBlocksLowerTriangular" | custom-call | tf_op jit(solution)/shard_map/triangular_solve/custom-call.0 | solution.py:56
  301.3 32.0 %all_gather.7 = bf16[2048,160]{0,1:T(8,128)(2,1)S(1)} all-gather(bf16[256,160]{0,1:T(8,128)(2,1)S(1)} %maximum_convert_fusion), channel_id=1, replica_groups=mesh['rows'=8,'cols'=4] {'rows'}, dimensions={0}, use_global_device_ids=true | all-gather | bytes 737280 | tf_op jit(solution)/shard_map/all_gather | solution.py:48
  333.3 1.3 copy.29
  334.7 19.8 %while.24 = (s32[]{:T(128)}, f32[8,128,160]{1,2,0:T(8,128)S(1)}, s32[]{:T(128)}, s32[320]{0:T(512)S(1)}, bf16[320,128,128]{2,1,0:T(8,128)(2,1)}, /*index=5*/s32[...) while((s32[]{:T(128)}, f32[8,128,160]{1,2,0:T(8,128)S(1)}, ...), condition=%wide.region_11.15_spmd, body=%wide.region_9.14_spmd.sunk | while | flops 169739648 | bytes 16258423 | solution.py:34
  335.4 3.3 gather_fusion.1
  338.7 2.8 fusion.72
  341.6 3.0 scatter_fusion.1
  345.3 3.3 gather_fusion.1
  348.6 2.8 fusion.72
  351.5 3.0 scatter_fusion.1
  355.7 108.8 %all-reduce.12.cloned.1.call-done = f32[1024,160]{0,1:T(8,128)} async-done(((f32[1024,160]{0,1:T(8,128)}), f32[1024,160]{0,1:T(8,128)}) %all-reduce.12.cloned.1.call-update) | async-done | bytes 655376 | tf_op jit(solution)/shard_map/psum | solution.py:50
  464.4 2.6 fusion.46
  467.1 71.1 %all-reduce.14.cloned.1.call-done = f32[160,160]{0,1:T(8,128)} async-done(((f32[160,160]{0,1:T(8,128)}), f32[160,160]{0,1:T(8,128)}) %all-reduce.14.cloned.1.call-update) | async-done | bytes 102416 | tf_op jit(solution)/shard_map/psum | solution.py:51
  540.3 11.7 %cholesky.174 = f32[128,128]{1,0:T(8,128)S(1)} custom-call(f32[128,128]{1,0:T(8,128)S(1)} %cholesky.211), custom_call_target="Cholesky" | custom-call | tf_op jit(solution)/shard_map/jit(cholesky)/cholesky | solution.py:55
  552.0 9.8 %custom-call.15 = f32[1,128,128]{1,2,0:T(8,128)S(1)} custom-call(f32[1,128,128]{2,1,0:T(8,128)S(1)} %get-tuple-element.176), custom_call_target="InvertDiagBlocksLowerTriangular" | custom-call | tf_op jit(solution)/shard_map/jit(cholesky)/cholesky | solution.py:55
  562.2 2.9 cholesky.194
  568.5 19.7 %custom-call.16 = f32[2,128,128]{1,2,0:T(8,128)S(1)} custom-call(f32[2,128,128]{2,1,0:T(8,128)S(1)} %pad_maximum_fusion.2), custom_call_target="InvertDiagBlocksLowerTriangular" | custom-call | tf_op jit(solution)/shard_map/triangular_solve/custom-call.0 | solution.py:56
  (67 shorter events, 20.9 us)
Async XLA Ops:
  7.2 168.5 %all-reduce.8.cloned.1.call-start = ((), (), s32[]{:S(2)}) async-start(), calls=%async_computation | async-start | bytes 1310720 | tf_op jit(solution)/shard_map/psum | solution.py:50
  65.0 184.6 %all-reduce.10.cloned.1.call-start = ((), (), s32[]{:S(2)}) async-start(), calls=%async_computation.1 | async-start | bytes 327680 | tf_op jit(solution)/shard_map/psum | solution.py:51
  178.3 286.1 %all-reduce.12.cloned.1.call-start = ((), (), s32[]{:S(2)}) async-start(), calls=%async_computation.2 | async-start | bytes 1310720 | tf_op jit(solution)/shard_map/psum | solution.py:50
  355.4 182.8 %all-reduce.14.cloned.1.call-start = ((), (), s32[]{:S(2)}) async-start(), calls=%async_computation.3 | async-start | bytes 327680 | tf_op jit(solution)/shard_map/psum | solution.py:51
Sparse Core Ops, SparseCore 0:
  65.1 110.4 all-reduce.7
  179.5 70.0 all-reduce.9
  355.5 108.8 all-reduce.11
  468.2 70.0 all-reduce.13
where the time goes:
time: 600 us; the launch traced here: 598 us
  waiting for transfers between devices  362 us (60%)
  other arithmetic  113 us (19%)
  blocking collectives  65.7 us (11%)
  matrix products  21.9 us (4%)
  local copies, waits for them, and re-layouts  17.8 us (3%)
  between operations  17.3 us (3%)
    psum x2, waiting for transfers between devices, shards(): whole = lax.psum(partial_value, 'cols')  219 us
    psum x2, waiting for transfers between devices, shards(): lax.psum(jnp.dot(whole.T, whole, precision=lax.Precision.HIGHEST), 'rows')  142 us
    all_gather x2, blocking collectives, shards(): gathered = lax.all_gather(current, 'rows', axis=0, tiled=True)  65.7 us
    another operation x14, other arithmetic, shards(): factor = jnp.linalg.cholesky(gram_matrix)  51.6 us
    another operation x11, other arithmetic, shards(): lax.linalg.triangular_solve(factor, owned, left_side=False, lower=True, t...  40.9 us
    gather x4, local copies, waits for them, and re-layouts, one_block(): picked = jnp.take(tile_stack, colids, axis=0)  13 us
  transfers between devices with their start and end apart: 4, of which 4 were waited for; matrix products, arithmetic and copies ran while one was open for 0% of the time, Pallas kernels for 0%

commit v1 on v0

--- a/solution.py
+++ b/solution.py
@@ -47,7 +47,7 @@
     for power in range(POWER):
         gathered = lax.all_gather(current, "rows", axis=0, tiled=True)
         partial_value = accumulate(own_values, own_rows, own_cols, own_count, gathered, RT)
-        whole = lax.psum(partial_value, "cols")
+        whole = jnp.sum(lax.all_gather(partial_value, "cols"), axis=0)
         gram_matrix = lax.psum(jnp.dot(whole.T, whole, precision=lax.Precision.HIGHEST), "rows")
         share_rows = whole.shape[0] // lax.axis_size("cols")
         owned = lax.dynamic_slice_in_dim(whole, lax.axis_index("cols") * share_rows, share_rows, 0)

time: 600 us -> 580 us (0.967)
  waiting for transfers between devices: 362 us -> 343 us
    psum x2 -> x0, waiting for transfers between devices: 219 us -> none  [shards(): whole = lax.psum(partial_value, 'cols')]
    all_gather x0 -> x2, waiting for transfers between devices: none -> 202 us  [shards(): whole = jnp.sum(lax.all_gather(partial_value, 'cols'), axis=0)]
where the time goes in v1:
time: 580 us; the launch traced here: 578 us
  waiting for transfers between devices  343 us (59%)
  other arithmetic  117 us (20%)
  blocking collectives  65.7 us (11%)
  local copies, waits for them, and re-layouts  18.6 us (3%)
  between operations  17.4 us (3%)
  matrix products  16 us (3%)
    all_gather x2, waiting for transfers between devices, shards(): whole = jnp.sum(lax.all_gather(partial_value, 'cols'), axis=0)  202 us
    psum x2, waiting for transfers between devices, shards(): lax.psum(jnp.dot(whole.T, whole, precision=lax.Precision.HIGHEST), 'rows')  141 us
    all_gather x2, blocking collectives, shards(): gathered = lax.all_gather(current, 'rows', axis=0, tiled=True)  65.7 us
    another operation x14, other arithmetic, shards(): factor = jnp.linalg.cholesky(gram_matrix)  51.6 us
    another operation x11, other arithmetic, shards(): lax.linalg.triangular_solve(factor, owned, left_side=False, lower=True, t...  40.9 us
    gather x4, local copies, waits for them, and re-layouts, one_block(): picked = jnp.take(tile_stack, colids, axis=0)  13 us
    scatter-add x4, other arithmetic, one_block(): return running.at[rowids].add(products * live_mask[:, None, None])  11.9 us
  transfers between devices with their start and end apart: 4, of which 4 were waited for; matrix products, arithmetic and copies ran while one was open for 0% of the time, Pallas kernels for 0%

profile of v1, /device:TPU:0, one launch (start us, length us, event | category | flops | bytes accessed | tf_op | source)
XLA Modules:
  0.0 578.4 jit_solution(5261142103797223321)
XLA Ops:
  9.3 33.6 %all_gather.12 = bf16[2048,160]{0,1:T(8,128)(2,1)S(1)} all-gather(bf16[256,160]{0,1:T(8,128)(2,1)} %param.18), channel_id=1, replica_groups=mesh['rows'=8,'cols'=4] {'rows'}, dimensions={0}, use_global_device_ids=true | all-gather | bytes 737280 | tf_op jit(solution)/shard_map/all_gather | solution.py:48
  44.2 19.8 %while.23 = (s32[]{:T(128)}, f32[8,128,160]{1,2,0:T(8,128)S(1)}, s32[]{:T(128)}, s32[320]{0:T(512)S(1)}, bf16[320,128,128]{2,1,0:T(8,128)(2,1)}, /*index=5*/s32[...) while((s32[]{:T(128)}, f32[8,128,160]{1,2,0:T(8,128)S(1)}, ...), condition=%wide.region_2.4_spmd, body=%wide.region_0.3_spmd.sunk | while | flops 169739648 | bytes 16258423 | solution.py:34
  45.0 3.3 gather_fusion
  48.3 2.8 fusion.67
  51.1 3.0 scatter_fusion
  54.9 3.3 gather_fusion
  58.1 2.8 fusion.67
  61.0 3.0 scatter_fusion
  65.5 102.1 %all-gather.3.cloned.1.call-done = f32[4,1024,160]{1,2,0:T(8,128)} async-done(((f32[1,1024,160]{1,2,0:T(8,128)}), f32[4,1024,160]{1,2,0:T(8,128)}) %all-gather.3.cloned.1.call-update) | async-done | bytes 2621456 | tf_op jit(solution)/shard_map/all_gather | solution.py:50
  167.6 2.0 reduce_sum.18
  169.6 1.4 fusion.45
  171.2 70.3 %all-reduce.6.cloned.1.call-done = f32[160,160]{0,1:T(8,128)} async-done(((f32[160,160]{0,1:T(8,128)}), f32[160,160]{0,1:T(8,128)}) %all-reduce.6.cloned.1.call-update) | async-done | bytes 102416 | tf_op jit(solution)/shard_map/psum | solution.py:51
  243.5 11.7 %cholesky.136 = f32[128,128]{1,0:T(8,128)S(1)} custom-call(f32[128,128]{1,0:T(8,128)S(1)} %cholesky.208), custom_call_target="Cholesky" | custom-call | tf_op jit(solution)/shard_map/jit(cholesky)/cholesky | solution.py:55
  255.2 9.8 %custom-call.13 = f32[1,128,128]{1,2,0:T(8,128)S(1)} custom-call(f32[1,128,128]{2,1,0:T(8,128)S(1)} %get-tuple-element.186), custom_call_target="InvertDiagBlocksLowerTriangular" | custom-call | tf_op jit(solution)/shard_map/jit(cholesky)/cholesky | solution.py:55
  265.4 2.9 cholesky.156
  271.2 19.7 %custom-call.14 = f32[2,128,128]{1,2,0:T(8,128)S(1)} custom-call(f32[2,128,128]{2,1,0:T(8,128)S(1)} %pad_maximum_fusion.1), custom_call_target="InvertDiagBlocksLowerTriangular" | custom-call | tf_op jit(solution)/shard_map/triangular_solve/custom-call.0 | solution.py:56
  291.6 32.0 %all_gather.14 = bf16[2048,160]{0,1:T(8,128)(2,1)S(1)} all-gather(bf16[256,160]{0,1:T(8,128)(2,1)S(1)} %maximum_convert_fusion), channel_id=1, replica_groups=mesh['rows'=8,'cols'=4] {'rows'}, dimensions={0}, use_global_device_ids=true | all-gather | bytes 737280 | tf_op jit(solution)/shard_map/all_gather | solution.py:48
  325.0 19.8 %while.24 = (s32[]{:T(128)}, f32[8,128,160]{1,2,0:T(8,128)S(1)}, s32[]{:T(128)}, s32[320]{0:T(512)S(1)}, bf16[320,128,128]{2,1,0:T(8,128)(2,1)}, /*index=5*/s32[...) while((s32[]{:T(128)}, f32[8,128,160]{1,2,0:T(8,128)S(1)}, ...), condition=%wide.region_11.15_spmd, body=%wide.region_9.14_spmd.sunk | while | flops 169739648 | bytes 16258423 | solution.py:34
  325.8 3.3 gather_fusion.1
  329.0 2.8 fusion.70
  331.9 3.0 scatter_fusion.1
  335.7 3.3 gather_fusion.1
  338.9 2.8 fusion.70
  341.8 3.0 scatter_fusion.1
  346.4 100.3 %all-gather.5.cloned.1.call-done = f32[4,1024,160]{1,2,0:T(8,128)} async-done(((f32[1,1024,160]{1,2,0:T(8,128)}), f32[4,1024,160]{1,2,0:T(8,128)}) %all-gather.5.cloned.1.call-update) | async-done | bytes 2621456 | tf_op jit(solution)/shard_map/all_gather | solution.py:50
  446.7 2.0 reduce_sum.19
  448.7 1.4 fusion.46
  450.1 70.4 %all-reduce.8.cloned.1.call-done = f32[160,160]{0,1:T(8,128)} async-done(((f32[160,160]{0,1:T(8,128)}), f32[160,160]{0,1:T(8,128)}) %all-reduce.8.cloned.1.call-update) | async-done | bytes 102416 | tf_op jit(solution)/shard_map/psum | solution.py:51
  522.5 11.7 %cholesky.174 = f32[128,128]{1,0:T(8,128)S(1)} custom-call(f32[128,128]{1,0:T(8,128)S(1)} %cholesky.211), custom_call_target="Cholesky" | custom-call | tf_op jit(solution)/shard_map/jit(cholesky)/cholesky | solution.py:55
  534.3 9.8 %custom-call.15 = f32[1,128,128]{1,2,0:T(8,128)S(1)} custom-call(f32[1,128,128]{2,1,0:T(8,128)S(1)} %get-tuple-element.184), custom_call_target="InvertDiagBlocksLowerTriangular" | custom-call | tf_op jit(solution)/shard_map/jit(cholesky)/cholesky | solution.py:55
  544.4 2.9 cholesky.194
  550.8 19.7 %custom-call.16 = f32[2,128,128]{1,2,0:T(8,128)S(1)} custom-call(f32[2,128,128]{2,1,0:T(8,128)S(1)} %pad_maximum_fusion.2), custom_call_target="InvertDiagBlocksLowerTriangular" | custom-call | tf_op jit(solution)/shard_map/triangular_solve/custom-call.0 | solution.py:56
  (71 shorter events, 21.1 us)
Async XLA Ops:
  7.2 160.4 %all-gather.3.cloned.1.call-start = ((), (), s32[]{:S(2)}) async-start(), calls=%async_computation | async-start | bytes 3276800 | tf_op jit(solution)/shard_map/all_gather | solution.py:50
  65.4 176.1 %all-reduce.6.cloned.1.call-start = ((), (), s32[]{:S(2)}) async-start(), calls=%async_computation.1 | async-start | bytes 327680 | tf_op jit(solution)/shard_map/psum | solution.py:51
  171.0 275.7 %all-gather.5.cloned.1.call-start = ((), (), s32[]{:S(2)}) async-start(), calls=%async_computation.2 | async-start | bytes 3276800 | tf_op jit(solution)/shard_map/all_gather | solution.py:50
  346.2 174.3 %all-reduce.8.cloned.1.call-start = ((), (), s32[]{:S(2)}) async-start(), calls=%async_computation.3 | async-start | bytes 327680 | tf_op jit(solution)/shard_map/psum | solution.py:51
Sparse Core Ops, SparseCore 0:
  65.5 102.0 all-gather.2
  171.5 69.9 all-reduce.5
  346.3 100.3 all-gather.4
  450.5 69.9 all-reduce.7
